TPU v7x, 32 devices: a whole 2x2x4 slice. The times are simulated.
32 devices in a mesh: shard: 2 (over x), ctx: 4 (over y, core), tp: 4 (over z).
Axes of the slice: x: 2, y: 2, z: 4, core: 2. Of those that a mesh axis runs over, the one named last changes fastest.
Arguments:
- tokens: bfloat16 [6, 608, 1024], P('shard', 'ctx'), may hold values from -6 to 6
- pad_mask: int32 [6, 608], P('shard', 'ctx'), may hold values from 0 to 1, as said below
- ln1_gain: float32 [1024], replicated, may hold values from 0.25 to 1.75
- ln1_shift: float32 [1024], replicated, may hold values from -3 to 3
- w_qkv: bfloat16 [3, 1024, 1024], P(None, 'shard', 'tp'), may hold values from -0.1875 to 0.1875
- b_qv: float32 [2, 1024], P(None, 'tp'), may hold values from -3 to 3
- w_out: bfloat16 [1024, 1024], P('tp', 'shard'), may hold values from -1 to 1
- b_out: float32 [1024], replicated, may hold values from -3 to 3
- ln2_gain: float32 [1024], replicated, may hold values from 0.25 to 1.75
- ln2_shift: float32 [1024], replicated, may hold values from -3 to 3
- w_up: bfloat16 [1024, 4096], P('shard', 'tp'), may hold values from -0.1875 to 0.1875
- b_up: float32 [4096], P('tp'), may hold values from -3 to 3
- w_down: bfloat16 [4096, 1024], P('tp', 'shard'), may hold values from -0.09375 to 0.09375
- b_down: float32 [1024], replicated, may hold values from -4 to 4
- cotangent: bfloat16 [6, 608, 1024], P('shard', 'ctx'), may hold values from -6 to 6
Outputs:
- out_tokens: float32 [6, 608, 1024], P('shard', 'ctx')
- grad_tokens: float32 [6, 608, 1024], P('shard', 'ctx')
- grad_w_qkv: float32 [3, 1024, 1024], P(None, 'shard', 'tp')
- grad_b_qv: float32 [2, 1024], P(None, 'tp')
- grad_w_out: float32 [1024, 1024], P('tp', 'shard')
- grad_b_out: float32 [1024], replicated
- grad_ln1_gain: float32 [1024], replicated
- grad_ln1_shift: float32 [1024], replicated
- grad_ln2_gain: float32 [1024], replicated
- grad_ln2_shift: float32 [1024], replicated
- grad_w_up: float32 [1024, 4096], P('shard', 'tp')
- grad_b_up: float32 [4096], P('tp')
- grad_w_down: float32 [4096, 1024], P('tp', 'shard')
- grad_b_down: float32 [1024], replicated
Inputs may be any that keep to these rules, and one draw needn't show every extreme that they name: `pad_mask`: each image has exactly 577 ones; the 31 padding slots may lie anywhere in the image.
All inputs are finite; a program needn't handle non-finite values.
Results may differ from a plain program's by a relative error of at most 0.02.
Values may be sent and summed in bfloat16 or wider, within the bound.
A program may use at most 128 MiB of HBM per device.

v0:
```python
import math
import jax
import jax.numpy as jnp
from jax import lax
from jax.sharding import PartitionSpec as P

HD = 64
NEG_FILL = -1e30


def normalize(values, gain, shift):
    row_mean = jnp.mean(values, axis=-1, keepdims=True)
    centred = values - row_mean
    inv_std = lax.rsqrt(jnp.mean(centred * centred, axis=-1, keepdims=True) + 1e-06)
    unit_rows = centred * inv_std
    return (unit_rows, inv_std, unit_rows * gain + shift)


def norm_back(upstream, unit_rows, inv_std, gain):
    scaled = upstream * gain
    centre = jnp.mean(scaled, axis=-1, keepdims=True)
    along = jnp.mean(scaled * unit_rows, axis=-1, keepdims=True)
    return inv_std * (scaled - centre - unit_rows * along)


def gelu_slope(pre_act):
    return (
        0.5 * (1.0 + lax.erf(pre_act * 0.7071067811865476))
        + pre_act * jnp.exp(-0.5 * pre_act * pre_act) * 0.3989422804014327
    )


def body(
    tokens,
    pad_mask,
    ln1_gain,
    ln1_shift,
    w_qkv,
    b_qv,
    w_out,
    b_out,
    ln2_gain,
    ln2_shift,
    w_up,
    b_up,
    w_down,
    b_down,
    cotangent,
):
    scale = 1.0 / math.sqrt(HD)
    images, piece, width = tokens.shape
    tok_count = images * piece
    qkv_full, out_full = (
        lax.all_gather(w_qkv, "shard", axis=1, tiled=True),
        lax.all_gather(w_out, "shard", axis=1, tiled=True),
    )
    up_full, down_full = (
        lax.all_gather(w_up, "shard", axis=0, tiled=True),
        lax.all_gather(w_down, "shard", axis=1, tiled=True),
    )
    local_width = out_full.shape[0]
    local_heads = local_width // HD
    inputs_wide = tokens.reshape(tok_count, width).astype(jnp.float32)
    first_unit, first_inv, first_norm = normalize(inputs_wide, ln1_gain, ln1_shift)
    first_low = first_norm.astype(jnp.bfloat16)
    projected = jnp.einsum("td,cdh->cth", first_low, qkv_full, preferred_element_type=jnp.float32)
    queries = (projected[0] + b_qv[0]).astype(jnp.bfloat16)
    key_local = projected[1].astype(jnp.bfloat16).reshape(images, piece, local_width)
    value_local = (projected[2] + b_qv[1]).astype(jnp.bfloat16).reshape(images, piece, local_width)
    valid_local = (pad_mask > 0).astype(jnp.bfloat16)
    key_all, value_all, valid_all = (
        lax.all_gather(key_local, "ctx", axis=1, tiled=True),
        lax.all_gather(value_local, "ctx", axis=1, tiled=True),
        lax.all_gather(valid_local, "ctx", axis=1, tiled=True),
    )
    seq_len = key_all.shape[1]
    query_heads = queries.reshape(images, piece, local_heads, HD)
    key_heads = key_all.reshape(images, seq_len, local_heads, HD)
    value_heads = value_all.reshape(images, seq_len, local_heads, HD)

    def masked_scores():
        scores = (
            jnp.einsum(
                "iqhe,ikhe->ihqk", query_heads, key_heads, preferred_element_type=jnp.float32
            )
            * scale
        )
        return jnp.where(valid_all[:, None, None, :] > 0.5, scores, NEG_FILL)

    scores = masked_scores()
    row_top = jnp.max(scores, axis=-1, keepdims=True)
    log_total = row_top + jnp.log(jnp.sum(jnp.exp(scores - row_top), axis=-1, keepdims=True))
    weights_low = jnp.exp(scores - log_total).astype(jnp.bfloat16)
    attended = jnp.einsum(
        "ihqk,ikhe->iqhe", weights_low, value_heads, preferred_element_type=jnp.float32
    )
    attended = attended.astype(jnp.bfloat16).reshape(tok_count, local_width)
    attn_part = jnp.dot(attended, out_full, preferred_element_type=jnp.float32)
    middle = (
        inputs_wide + lax.psum(attn_part.astype(jnp.bfloat16), "tp").astype(jnp.float32) + b_out
    )
    second_unit, second_inv, second_norm = normalize(middle, ln2_gain, ln2_shift)
    second_low = second_norm.astype(jnp.bfloat16)
    pre_act = jnp.dot(second_low, up_full, preferred_element_type=jnp.float32) + b_up
    activated = jax.nn.gelu(pre_act, approximate=False).astype(jnp.bfloat16)
    mlp_part = jnp.dot(activated, down_full, preferred_element_type=jnp.float32)
    result = middle + lax.psum(mlp_part.astype(jnp.bfloat16), "tp").astype(jnp.float32) + b_down
    out_tokens = result.reshape(images, piece, width)
    upstream_low = cotangent.reshape(tok_count, width)
    upstream_wide = upstream_low.astype(jnp.float32)
    act_grad = jnp.dot(upstream_low, down_full.T, preferred_element_type=jnp.float32) * gelu_slope(
        pre_act
    )
    act_low = act_grad.astype(jnp.bfloat16)
    grad_down = jnp.einsum("tf,td->fd", activated, upstream_low, preferred_element_type=jnp.float32)
    grad_up = jnp.einsum("td,tf->df", second_low, act_low, preferred_element_type=jnp.float32)
    norm2_part = jnp.dot(act_low, up_full.T, preferred_element_type=jnp.float32)
    norm2_grad = lax.psum(norm2_part.astype(jnp.bfloat16), "tp").astype(jnp.float32)
    middle_grad = upstream_wide + norm_back(norm2_grad, second_unit, second_inv, ln2_gain)
    middle_low = middle_grad.astype(jnp.bfloat16)
    grad_out = jnp.einsum("th,td->hd", attended, middle_low, preferred_element_type=jnp.float32)
    attended_grad = jnp.dot(middle_low, out_full.T, preferred_element_type=jnp.float32)
    attended_grad = attended_grad.astype(jnp.bfloat16).reshape(images, piece, local_heads, HD)
    weights = jnp.exp(masked_scores() - log_total)
    weights_low = weights.astype(jnp.bfloat16)
    weight_grad = jnp.einsum(
        "iqhe,ikhe->ihqk", attended_grad, value_heads, preferred_element_type=jnp.float32
    )
    row_dot = jnp.sum(weights * weight_grad, axis=-1, keepdims=True)
    score_grad = (scale * weights * (weight_grad - row_dot)).astype(jnp.bfloat16)
    query_grad = jnp.einsum(
        "ihqk,ikhe->iqhe", score_grad, key_heads, preferred_element_type=jnp.float32
    ).reshape(tok_count, local_width)
    key_part = jnp.einsum(
        "ihqk,iqhe->ikhe", score_grad, query_heads, preferred_element_type=jnp.float32
    ).reshape(images, seq_len, local_width)
    value_part = jnp.einsum(
        "ihqk,iqhe->ikhe", weights_low, attended_grad, preferred_element_type=jnp.float32
    ).reshape(images, seq_len, local_width)
    key_grad, value_grad = (
        lax.psum_scatter(
            key_part.astype(jnp.bfloat16), "ctx", scatter_dimension=1, tiled=True
        ).astype(jnp.float32),
        lax.psum_scatter(
            value_part.astype(jnp.bfloat16), "ctx", scatter_dimension=1, tiled=True
        ).astype(jnp.float32),
    )
    key_grad = key_grad.reshape(tok_count, local_width)
    value_grad = value_grad.reshape(tok_count, local_width)
    proj_grad = jnp.stack([query_grad, key_grad, value_grad]).astype(jnp.bfloat16)
    grad_qkv = jnp.einsum("td,cth->cdh", first_low, proj_grad, preferred_element_type=jnp.float32)
    norm1_part = jnp.einsum("cth,cdh->td", proj_grad, qkv_full, preferred_element_type=jnp.float32)
    norm1_grad = lax.psum(norm1_part.astype(jnp.bfloat16), "tp").astype(jnp.float32)
    input_grad = middle_grad + norm_back(norm1_grad, first_unit, first_inv, ln1_gain)
    grad_tokens = input_grad.reshape(images, piece, width)
    small = lax.psum(
        (
            jnp.stack([jnp.sum(query_grad, axis=0), jnp.sum(value_grad, axis=0)]),
            jnp.sum(middle_grad, axis=0),
            jnp.sum(norm1_grad * first_unit, axis=0),
            jnp.sum(norm1_grad, axis=0),
            jnp.sum(norm2_grad * second_unit, axis=0),
            jnp.sum(norm2_grad, axis=0),
            jnp.sum(act_grad, axis=0),
            jnp.sum(upstream_wide, axis=0),
        ),
        ("shard", "ctx"),
    )
    summed = (
        lax.psum(grad_qkv.astype(jnp.bfloat16), "ctx").astype(jnp.float32),
        lax.psum(grad_out.astype(jnp.bfloat16), "ctx").astype(jnp.float32),
        lax.psum(grad_up.astype(jnp.bfloat16), "ctx").astype(jnp.float32),
        lax.psum(grad_down.astype(jnp.bfloat16), "ctx").astype(jnp.float32),
    )
    big_sums = (
        lax.psum_scatter(
            summed[0].astype(jnp.bfloat16), "shard", scatter_dimension=1, tiled=True
        ).astype(jnp.float32),
        lax.psum_scatter(
            summed[1].astype(jnp.bfloat16), "shard", scatter_dimension=1, tiled=True
        ).astype(jnp.float32),
        lax.psum_scatter(
            summed[2].astype(jnp.bfloat16), "shard", scatter_dimension=0, tiled=True
        ).astype(jnp.float32),
        lax.psum_scatter(
            summed[3].astype(jnp.bfloat16), "shard", scatter_dimension=1, tiled=True
        ).astype(jnp.float32),
    )
    return (
        out_tokens,
        grad_tokens,
        big_sums[0],
        small[0],
        big_sums[1],
        small[1],
        small[2],
        small[3],
        small[4],
        small[5],
        big_sums[2],
        small[6],
        big_sums[3],
        small[7],
    )


def solution(mesh):
    return jax.shard_map(
        body,
        mesh=mesh,
        in_specs=(
            P("shard", "ctx", None),
            P("shard", "ctx"),
            P(),
            P(),
            P(None, "shard", "tp"),
            P(None, "tp"),
            P("tp", "shard"),
            P(),
            P(),
            P(),
            P("shard", "tp"),
            P("tp"),
            P("tp", "shard"),
            P(),
            P("shard", "ctx", None),
        ),
        out_specs=(
            P("shard", "ctx", None),
            P("shard", "ctx", None),
            P(None, "shard", "tp"),
            P(None, "tp"),
            P("tp", "shard"),
            P(),
            P(),
            P(),
            P(),
            P(),
            P("shard", "tp"),
            P("tp"),
            P("tp", "shard"),
            P(),
        ),
        check_vma=False,
    )
```

profile of v0, /device:TPU:0, one launch (start us, length us, event | category | flops | bytes accessed | tf_op | source)
XLA Modules:
  0.0 626.5 jit_solution(8793724352426675898)
XLA Ops:
  10.9 6.2 all-gather
  17.2 14.5 %all_gather.25 = bf16[256,1024]{1,0:T(8,128)(2,1)S(1)} all-gather(bf16[256,512]{1,0:T(8,128)(2,1)S(1)} %copy-done.19), channel_id=1, replica_groups=mesh['shard'=2,'ctx'=4,'tp'=4] {'shard'}, dimensions={1}, use_global_device_ids=true | all-gather | bytes 786432 | tf_op jit(solution)/shard_map/all_gather | solution.py:55
  33.4 10.4 %all-gather.5.cloned.1.call-done = bf16[3,1024,256]{2,1,0:T(8,128)(2,1)} async-done(((bf16[3,512,256]{2,1,0:T(8,128)(2,1)}), bf16[3,1024,256]{2,1,0:T(8,128)(2,1)}) %all-gather.5.cloned.1.call-update) | async-done | bytes 1572880 | tf_op jit(solution)/shard_map/all_gather | solution.py:54
  51.3 11.4 %all_gather.24 = bf16[3,608,256]{2,1,0:T(8,128)(2,1)} all-gather(bf16[3,152,256]{2,1,0:T(8,128)(2,1)} %bitcast.92), channel_id=1, replica_groups=mesh['shard'=2,'ctx'=4,'tp'=4] {'ctx'}, dimensions={1}, use_global_device_ids=true | all-gather | bytes 1167360 | tf_op jit(solution)/shard_map/all_gather | solution.py:72
  64.3 10.0 %all_gather.22 = bf16[3,608,256]{2,1,0:T(8,128)(2,1)} all-gather(bf16[3,152,256]{2,1,0:T(8,128)(2,1)S(1)} %add_convert_fusion.3), channel_id=1, replica_groups=mesh['shard'=2,'ctx'=4,'tp'=4] {'ctx'}, dimensions={1}, use_global_device_ids=true | all-gather | bytes 1167360 | tf_op jit(solution)/shard_map/all_gather | solution.py:73
  84.5 47.4 %all-reduce.12.cloned.1.call-done = bf16[456,1024]{1,0:T(8,128)(2,1)} async-done(((bf16[456,1024]{1,0:T(8,128)(2,1)}), bf16[456,1024]{1,0:T(8,128)(2,1)}) %all-reduce.12.cloned.1.call-update) | async-done | bytes 933904 | tf_op jit(solution)/shard_map/psum | solution.py:100
  135.1 30.7 %all-gather.7.cloned.1.call-done = bf16[1024,1024]{1,0:T(8,128)(2,1)} async-done(((bf16[512,1024]{1,0:T(8,128)(2,1)}), bf16[1024,1024]{1,0:T(8,128)(2,1)}) %all-gather.7.cloned.1.call-update) | async-done | bytes 2097168 | tf_op jit(solution)/shard_map/all_gather | solution.py:58
  165.8 7.8 %fusion.18 = (bf16[456,1024]{1,0:T(8,128)(2,1)}, f32[456,1024]{1,0:T(8,128)}) fusion(f32[1024]{0:T(1024)S(1)} %copy-done.28, bf16[1024,1024]{1,0:T(8,128)(2,1)} %all-gather.7.cloned.1.call-done, f32[456,1024]{1,0:T(8,128)S(1)} %subtract_multiply_fusion, f32[1024]{0:T(1024)S(1)} %copy-done.29, f32[1024]{0:T(1024)S(1)} %copy-done.22), kind=kOutput, calls=%fused_computation.33 | convolution fusion | flops 988520448 | bytes 6778880 | tf_op jit(solution)/shard_map/dot_general | solution.py:104
  173.6 26.7 %all-gather.9.cloned.1.call-done = bf16[1024,1024]{1,0:T(8,128)(2,1)} async-done(((bf16[1024,512]{1,0:T(8,128)(2,1)}), bf16[1024,1024]{1,0:T(8,128)(2,1)}) %all-gather.9.cloned.1.call-update) | async-done | bytes 2097168 | tf_op jit(solution)/shard_map/all_gather | solution.py:59
  200.3 4.3 fusion.57
  207.7 48.7 %all-reduce.14.cloned.1.call-done = bf16[456,1024]{1,0:T(8,128)(2,1)} async-done(((bf16[456,1024]{1,0:T(8,128)(2,1)}), bf16[456,1024]{1,0:T(8,128)(2,1)}) %all-reduce.14.cloned.1.call-update) | async-done | bytes 933904 | tf_op jit(solution)/shard_map/psum | solution.py:118
  264.0 4.8 convolution_convert_fusion.3
  268.8 5.0 multiply_reduce_fusion
  277.1 4.5 multiply_convert_fusion
  288.4 4.4 convolution_convert_fusion.1
  304.3 39.7 %all-reduce.20.cloned.1.call-done = (bf16[3,608,256]{2,0,1:T(4,128)(2,1)}, bf16[3,608,256]{2,0,1:T(4,128)(2,1)}) async-done(((bf16[3,608,256]{2,0,1:T(4,128)(2,1)}, bf16[3,608,256]{2,0,1:T(4,128)(2,1)}), (bf16[3,608,256]{2,0,1:T(4,128)(2,1)}, bf16[3,608,256]{2,0,1:T(4,128)(2,1)})) %all-reduce.20.cloned.1.call-update) | async-done | bytes 1867792
  354.7 6.7 %reduce-scatter.7.cloned.1.call-done = bf16[256,512]{1,0:T(8,128)(2,1)} async-done(((bf16[256,1024]{1,0:T(8,128)(2,1)}), bf16[256,512]{1,0:T(8,128)(2,1)}) %reduce-scatter.7.cloned.1.call-update) | async-done | bytes 262160 | tf_op jit(solution)/shard_map/reduce_scatter | solution.py:179
  361.5 34.8 %reduce-scatter.9.cloned.1.call-done = bf16[512,1024]{1,0:T(8,128)(2,1)} async-done(((bf16[1024,1024]{1,0:T(8,128)(2,1)}), bf16[512,1024]{1,0:T(8,128)(2,1)}) %reduce-scatter.9.cloned.1.call-update) | async-done | bytes 1048592 | tf_op jit(solution)/shard_map/reduce_scatter | solution.py:182
  396.2 34.8 %reduce-scatter.11.cloned.1.call-done = bf16[1024,512]{1,0:T(8,128)(2,1)} async-done(((bf16[1024,1024]{1,0:T(8,128)(2,1)}), bf16[1024,512]{1,0:T(8,128)(2,1)}) %reduce-scatter.11.cloned.1.call-update) | async-done | bytes 1048592 | tf_op jit(solution)/shard_map/reduce_scatter | solution.py:185
  431.0 28.8 %reduce-scatter.5.cloned.1.call-done = bf16[3,512,256]{1,2,0:T(8,128)(2,1)} async-done(((bf16[3,1024,256]{1,2,0:T(8,128)(2,1)}), bf16[3,512,256]{1,2,0:T(8,128)(2,1)}) %reduce-scatter.5.cloned.1.call-update) | async-done | bytes 786448 | tf_op jit(solution)/shard_map/reduce_scatter | solution.py:176
  461.3 80.3 %all-reduce.16.cloned.1.call-done = (bf16[456,1024]{1,0:T(8,128)(2,1)}, bf16[456,1024]{1,0:T(8,128)(2,1)}) async-done(((bf16[456,1024]{1,0:T(8,128)(2,1)}, bf16[456,1024]{1,0:T(8,128)(2,1)}), (bf16[456,1024]{1,0:T(8,128)(2,1)}, bf16[456,1024]{1,0:T(8,128)(2,1)})) %all-reduce.16.cloned.1.call-update) | async-done | bytes 1867792 | tf_op jit(solution)/shard_map/psum | solution.py:107
  544.4 24.2 %all-reduce.2 = (f32[2,256]{1,0:T(2,128)}, f32[1024]{0:T(1024)}, f32[1024]{0:T(1024)}, f32[1024]{0:T(1024)}, f32[1024]{0:T(1024)}, /*index=5*/f32[1024]{0:T(1024)}, f32[1024]{0:T(1024)}, f32[1024]{0:T(1024)}) all-reduce(f32[2,256]{1,0:T(2,128)S(1)} %pad_maximum_fusion.3, ...), channel_id=1, replica_groups=mesh['shard'=2,'ctx'=4,'tp'=4] {'shard','ctx'}, use_global_device_ids=true, to_apply=%region_21.22 | all-reduce | flops 7680 | bytes 61440 | tf_op jit(solution)/shard_map/psum | solution.py:156
  568.6 4.5 fusion.10
  573.1 38.9 %all-reduce.18.cloned.1.call-done = (bf16[3,512,256]{1,2,0:T(8,128)(2,1)}, bf16[256,512]{1,0:T(8,128)(2,1)}, bf16[512,1024]{1,0:T(8,128)(2,1)}, bf16[1024,512]{1,0:T(8,128)(2,1)}) async-done(((bf16[3,512,256]{1,2,0:T(8,128)(2,1)}, bf16[256,512]{1,0:T(8,128)(2,1)}, bf16[512,1024]{1,0:T(8,128)(2,1)}, bf16[1024,512]{1,0:T(8,128)(2,1)}), (bf16[3,512,256]{1,2,0:T(8,128)(2,1)}, bf16[256,512]{1,0:T(8,128)(2,1)}, ...) | async-done | bytes 3145744 | tf_op jit(solution)/shard_map/psum | solution.py:170
  (155 shorter events, 81.8 us)
Async XLA Ops:
  7.2 10.0 %copy-start.19 = (bf16[256,512]{1,0:T(8,128)(2,1)S(1)}, bf16[256,512]{1,0:T(8,128)(2,1)}, u32[]{:S(2)}) copy-start(bf16[256,512]{1,0:T(8,128)(2,1)} %param.21) | copy-start | bytes 786436
  7.2 24.5 %copy-start.21 = (f32[1024]{0:T(1024)S(1)}, f32[1024]{0:T(1024)}, u32[]{:S(2)}) copy-start(f32[1024]{0:T(1024)} %param.17) | copy-start | bytes 12292
  7.2 24.5 %copy-start.25 = (f32[1024]{0:T(1024)S(1)}, f32[1024]{0:T(1024)}, u32[]{:S(2)}) copy-start(f32[1024]{0:T(1024)} %param.18) | copy-start | bytes 12292
  7.2 36.5 %all-gather.5.cloned.1.call-start = ((), (), s32[]{:S(2)}) async-start(), calls=%async_computation.4 | async-start | bytes 2359296 | tf_op jit(solution)/shard_map/all_gather | solution.py:54
  8.0 124.0 %all-reduce.12.cloned.1.call-start = ((), (), s32[]{:S(2)}) async-start(), calls=%async_computation.5 | async-start | bytes 1867776 | tf_op jit(solution)/shard_map/psum | solution.py:100
  33.3 12.7 %copy-start.17 = (bf16[456,1024]{1,0:T(8,128)(2,1)}, bf16[456,1024]{1,0:T(8,128)(2,1)S(1)}, u32[]{:S(2)}) copy-start(bf16[456,1024]{1,0:T(8,128)(2,1)S(1)} %get-tuple-element.101) | copy-start | bytes 2801668
  51.2 25.2 %copy-start.6 = (bf16[3,152,4,64]{1,3,2,0:T(8,128)(2,1)}, bf16[3,152,4,64]{1,3,2,0:T(8,128)(2,1)S(1)}, u32[]{:S(2)}) copy-start(bf16[3,152,4,64]{1,3,2,0:T(8,128)(2,1)S(1)} %copy.66) | copy-start | bytes 700420
  64.2 12.2 %copy-start.4 = (bf16[3,608,256]{1,2,0:T(8,128)(2,1)}, bf16[3,608,256]{1,2,0:T(8,128)(2,1)S(1)}, u32[]{:S(2)}) copy-start(bf16[3,608,256]{1,2,0:T(8,128)(2,1)S(1)} %copy.65) | copy-start | bytes 2801668
  83.0 82.8 %all-gather.7.cloned.1.call-start = ((), (), s32[]{:S(2)}) async-start(), calls=%async_computation.6 | async-start | bytes 3145728 | tf_op jit(solution)/shard_map/all_gather | solution.py:58
  83.7 116.6 %all-gather.9.cloned.1.call-start = ((), (), s32[]{:S(2)}) async-start(), calls=%async_computation.7 | async-start | bytes 3145728 | tf_op jit(solution)/shard_map/all_gather | solution.py:59
  84.3 49.2 %copy-start.20 = (f32[1024]{0:T(1024)S(1)}, f32[1024]{0:T(1024)}, u32[]{:S(2)}) copy-start(f32[1024]{0:T(1024)} %param.22) | copy-start | bytes 12292
  84.3 172.1 %all-reduce.14.cloned.1.call-start = ((), (), s32[]{:S(2)}) async-start(), calls=%async_computation.8 | async-start | bytes 1867776 | tf_op jit(solution)/shard_map/psum | solution.py:118
  134.7 31.1 %copy-start.22 = (f32[1024]{0:T(1024)S(1)}, f32[1024]{0:T(1024)}, u32[]{:S(2)}) copy-start(f32[1024]{0:T(1024)} %param.23) | copy-start | bytes 12292
  134.7 31.1 %copy-start.28 = (f32[1024]{0:T(1024)S(1)}, f32[1024]{0:T(1024)}, u32[]{:S(2)}) copy-start(f32[1024]{0:T(1024)} %param.26) | copy-start | bytes 12292
  134.7 31.1 %copy-start.29 = (f32[1024]{0:T(1024)S(1)}, f32[1024]{0:T(1024)}, u32[]{:S(2)}) copy-start(f32[1024]{0:T(1024)} %param.24) | copy-start | bytes 12292
  135.1 121.4 %copy-start.3 = (f32[456,1024]{1,0:T(8,128)}, f32[456,1024]{1,0:T(8,128)S(1)}, u32[]{:S(2)}) copy-start(f32[456,1024]{1,0:T(8,128)S(1)} %subtract_multiply_fusion) | copy-start | bytes 5603332
  207.6 136.3 %all-reduce.20.cloned.1.call-start = ((), (), s32[]{:S(2)}) async-start(), calls=%async_computation.15 | async-start | bytes 4980736
  286.8 74.7 %reduce-scatter.7.cloned.1.call-start = ((), (), s32[]{:S(2)}) async-start(), calls=%async_computation.10 | async-start | bytes 786432 | tf_op jit(solution)/shard_map/reduce_scatter | solution.py:179
  288.4 107.9 %reduce-scatter.9.cloned.1.call-start = ((), (), s32[]{:S(2)}) async-start(), calls=%async_computation.11 | async-start | bytes 3145728 | tf_op jit(solution)/shard_map/reduce_scatter | solution.py:182
  292.8 138.2 %reduce-scatter.11.cloned.1.call-start = ((), (), s32[]{:S(2)}) async-start(), calls=%async_computation.12 | async-start | bytes 3145728 | tf_op jit(solution)/shard_map/reduce_scatter | solution.py:185
  297.0 162.8 %reduce-scatter.5.cloned.1.call-start = ((), (), s32[]{:S(2)}) async-start(), calls=%async_computation.9 | async-start | bytes 2359296 | tf_op jit(solution)/shard_map/reduce_scatter | solution.py:176
  348.7 192.9 %all-reduce.16.cloned.1.call-start = ((), (), s32[]{:S(2)}) async-start(), calls=%async_computation.13 | async-start | bytes 3735552 | tf_op jit(solution)/shard_map/psum | solution.py:107
  354.7 257.3 %all-reduce.18.cloned.1.call-start = ((), (), s32[]{:S(2)}) async-start(), calls=%async_computation.14 | async-start | bytes 6291456 | tf_op jit(solution)/shard_map/psum | solution.py:170
  541.6 27.0 %copy-start.23 = (f32[1024]{0:T(1024)S(1)}, f32[1024]{0:T(1024)}, u32[]{:S(2)}) copy-start(f32[1024]{0:T(1024)} %param.28) | copy-start | bytes 12292
  (20 other events, 57.9 us)
Sparse Core Ops, SparseCore 0:
  9.6 34.1 all-gather.4
  83.1 48.8 all-reduce.11
  133.5 32.2 all-gather.6
  167.2 33.0 all-gather.8
  207.8 48.6 all-reduce.13
  286.9 56.9 all-reduce.19
  346.7 14.6 reduce-scatter.6
  364.3 31.8 reduce-scatter.8
  399.0 31.8 reduce-scatter.10
  433.6 26.1 reduce-scatter.4
  462.8 78.6 all-reduce.15
  544.0 67.9 all-reduce.17
where the time goes:
time: 628 us; the launch traced here: 627 us
  waiting for transfers between devices  430 us (68%)
  blocking collectives  66.3 us (11%)
  matrix products  54.6 us (9%)
  other arithmetic  32.1 us (5%)
  local copies, waits for them, and re-layouts  27.5 us (4%)
  between operations  15.3 us (2%)
    psum x1, waiting for transfers between devices, body(): lax.psum(mlp_part.astype(jnp.bfloat16), 'tp').astype(jnp.float32)  80.3 us
    psum x1, waiting for transfers between devices, body(): lax.psum(norm2_part.astype(jnp.bfloat16), 'tp').astype(jnp.float32)  48.7 us
    psum x1, waiting for transfers between devices, body(): lax.psum(attn_part.astype(jnp.bfloat16), 'tp').astype(jnp.float32)  47.4 us
    unnamed x13, waiting for transfers between devices  41.7 us
    psum x1, waiting for transfers between devices, body(): lax.psum(grad_qkv.astype(jnp.bfloat16), 'ctx').astype(jnp.float32)  38.9 us
    reduce_scatter x1, waiting for transfers between devices, body(): lax.psum_scatter(summed[3].astype(jnp.bfloat16), 'shard', scatter_dimensi...  34.8 us
    reduce_scatter x1, waiting for transfers between devices, body(): lax.psum_scatter(summed[2].astype(jnp.bfloat16), 'shard', scatter_dimensi...  34.8 us
    all_gather x1, waiting for transfers between devices, body(): lax.all_gather(w_up, 'shard', axis=0, tiled=True)  30.7 us
  transfers between devices with their start and end apart: 12, of which 12 were waited for; matrix products, arithmetic and copies ran while one was open for 8% of the time, Pallas kernels for 0%

commit v1 on v0

--- a/solution.py
+++ b/solution.py
@@ -6,6 +6,18 @@
 
 HD = 64
 NEG_FILL = -1e30
+
+
+def collect(x, axis, dim):
+    ways, here, turn = (lax.axis_size(axis), lax.axis_index(axis), x.shape[dim])
+    line, have = (x, 1)
+    while have < ways:
+        line = jnp.concatenate(
+            [line, lax.ppermute(line, axis, [(d, (d - have) % ways) for d in range(ways)])],
+            axis=dim,
+        )
+        have = 2 * have
+    return jnp.roll(line, here * turn, axis=dim)
 
 
 def normalize(values, gain, shift):
@@ -56,7 +68,7 @@
     )
     up_full, down_full = (
         lax.all_gather(w_up, "shard", axis=0, tiled=True),
-        lax.all_gather(w_down, "shard", axis=1, tiled=True),
+        collect(w_down, "shard", 1),
     )
     local_width = out_full.shape[0]
     local_heads = local_width // HD

time: 628 us -> 598 us (0.952)
  waiting for transfers between devices: 430 us -> 397 us
    psum x1, waiting for transfers between devices: 47.4 us -> 19.2 us  [body(): lax.psum(attn_part.astype(jnp.bfloat16), 'tp').astype(jnp.float32)]
    all_gather x1 -> x0, waiting for transfers between devices: 26.7 us -> none  [body(): lax.all_gather(w_down, 'shard', axis=1, tiled=True)]
    ppermute x0 -> x1, waiting for transfers between devices: none -> 23.8 us  [collect(): lax.ppermute(line, axis, [(d, (d - have) % ways) for d in range(ways)])]
    unnamed x13 -> x12, waiting for transfers between devices: 41.7 us -> 40.6 us
where the time goes in v1:
time: 598 us; the launch traced here: 597 us
  waiting for transfers between devices  397 us (66%)
  blocking collectives  66.3 us (11%)
  matrix products  52.1 us (9%)
  other arithmetic  36.2 us (6%)
  local copies, waits for them, and re-layouts  27.7 us (5%)
  between operations  15 us (3%)
    psum x1, waiting for transfers between devices, body(): lax.psum(mlp_part.astype(jnp.bfloat16), 'tp').astype(jnp.float32)  80.7 us
    psum x1, waiting for transfers between devices, body(): lax.psum(norm2_part.astype(jnp.bfloat16), 'tp').astype(jnp.float32)  48.5 us
    unnamed x12, waiting for transfers between devices  40.6 us
    psum x1, waiting for transfers between devices, body(): lax.psum(grad_qkv.astype(jnp.bfloat16), 'ctx').astype(jnp.float32)  39.1 us
    reduce_scatter x1, waiting for transfers between devices, body(): lax.psum_scatter(summed[2].astype(jnp.bfloat16), 'shard', scatter_dimensi...  34.8 us
    reduce_scatter x1, waiting for transfers between devices, body(): lax.psum_scatter(summed[3].astype(jnp.bfloat16), 'shard', scatter_dimensi...  34.2 us
    all_gather x1, waiting for transfers between devices, body(): lax.all_gather(w_up, 'shard', axis=0, tiled=True)  30.7 us
    reduce_scatter x1, waiting for transfers between devices, body(): lax.psum_scatter(summed[0].astype(jnp.bfloat16), 'shard', scatter_dimensi...  29 us
  transfers between devices with their start and end apart: 12, of which 12 were waited for; matrix products, arithmetic and copies ran while one was open for 8% of the time, Pallas kernels for 0%

profile of v1, /device:TPU:0, one launch (start us, length us, event | category | flops | bytes accessed | tf_op | source)
XLA Modules:
  0.0 597.1 jit_solution(2427344567071403338)
XLA Ops:
  10.9 6.2 %all-gather = bf16[4,152,3]{1,2,0:T(4,128)(2,1)S(1)} all-gather(bf16[1,152,3]{1,2,0:T(4,128)(2,1)S(1)} %fusion.49), channel_id=1, replica_groups=mesh['shard'=2,'ctx'=4,'tp'=4] {'ctx'}, dimensions={0}, use_global_device_ids=true | all-gather | bytes 4560 | tf_op jit(solution)/shard_map/all_gather | solution.py:86
  17.2 14.5 %all_gather.22 = bf16[256,1024]{1,0:T(8,128)(2,1)S(1)} all-gather(bf16[256,512]{1,0:T(8,128)(2,1)S(1)} %copy-done.22), channel_id=1, replica_groups=mesh['shard'=2,'ctx'=4,'tp'=4] {'shard'}, dimensions={1}, use_global_device_ids=true | all-gather | bytes 786432 | tf_op jit(solution)/shard_map/all_gather | solution.py:67
  33.3 10.4 %all-gather.4.cloned.1.call-done = bf16[3,1024,256]{2,1,0:T(8,128)(2,1)} async-done(((bf16[3,512,256]{2,1,0:T(8,128)(2,1)}), bf16[3,1024,256]{2,1,0:T(8,128)(2,1)}) %all-gather.4.cloned.1.call-update) | async-done | bytes 1572880 | tf_op jit(solution)/shard_map/all_gather | solution.py:66
  51.3 11.4 %all_gather.21 = bf16[3,608,256]{2,1,0:T(8,128)(2,1)} all-gather(bf16[3,152,256]{2,1,0:T(8,128)(2,1)} %bitcast.94), channel_id=1, replica_groups=mesh['shard'=2,'ctx'=4,'tp'=4] {'ctx'}, dimensions={1}, use_global_device_ids=true | all-gather | bytes 1167360 | tf_op jit(solution)/shard_map/all_gather | solution.py:84
  64.3 10.0 %all_gather.19 = bf16[3,608,256]{2,1,0:T(8,128)(2,1)} all-gather(bf16[3,152,256]{2,1,0:T(8,128)(2,1)S(1)} %add_convert_fusion.3), channel_id=1, replica_groups=mesh['shard'=2,'ctx'=4,'tp'=4] {'ctx'}, dimensions={1}, use_global_device_ids=true | all-gather | bytes 1167360 | tf_op jit(solution)/shard_map/all_gather | solution.py:85
  85.0 23.8 %collective-permute-done = bf16[1024,512]{1,0:T(8,128)(2,1)} collective-permute-done((bf16[1024,512]{1,0:T(8,128)(2,1)S(1)}, bf16[1024,512]{1,0:T(8,128)(2,1)}, u32[]{:S(2)}, u32[]{:S(2)}) %collective-permute-start) | collective-permute-done | bytes 1048608 | tf_op jit(solution)/shard_map/ppermute | solution.py:16
  112.9 19.2 %all-reduce.12.cloned.1.call-done = bf16[456,1024]{1,0:T(8,128)(2,1)} async-done(((bf16[456,1024]{1,0:T(8,128)(2,1)}), bf16[456,1024]{1,0:T(8,128)(2,1)}) %all-reduce.12.cloned.1.call-update) | async-done | bytes 933904 | tf_op jit(solution)/shard_map/psum | solution.py:112
  135.2 30.7 %all-gather.6.cloned.1.call-done = bf16[1024,1024]{1,0:T(8,128)(2,1)} async-done(((bf16[512,1024]{1,0:T(8,128)(2,1)}), bf16[1024,1024]{1,0:T(8,128)(2,1)}) %all-gather.6.cloned.1.call-update) | async-done | bytes 2097168 | tf_op jit(solution)/shard_map/all_gather | solution.py:70
  165.9 7.7 %fusion.21 = (bf16[456,1024]{1,0:T(8,128)(2,1)}, f32[456,1024]{1,0:T(8,128)S(1)}) fusion(f32[1024]{0:T(1024)S(1)} %copy-done.31, bf16[1024,1024]{1,0:T(8,128)(2,1)} %all-gather.6.cloned.1.call-done, f32[456,1024]{1,0:T(8,128)S(1)} %subtract_multiply_fusion, f32[1024]{0:T(1024)S(1)} %copy-done.32, f32[1024]{0:T(1024)S(1)} %copy-done.25), kind=kOutput, calls=%fused_computation.40 | convolution fusion | flops 988520448 | bytes 6778880 | tf_op jit(solution)/shard_map/dot_general | solution.py:116
  178.9 48.5 %all-reduce.14.cloned.1.call-done = bf16[456,1024]{1,0:T(8,128)(2,1)} async-done(((bf16[456,1024]{1,0:T(8,128)(2,1)}), bf16[456,1024]{1,0:T(8,128)(2,1)}) %all-reduce.14.cloned.1.call-update) | async-done | bytes 933904 | tf_op jit(solution)/shard_map/psum | solution.py:130
  235.0 4.8 convolution_convert_fusion.3
  239.8 4.9 multiply_reduce_fusion
  248.1 4.5 multiply_convert_fusion
  259.1 4.4 convolution_convert_fusion.1
  263.6 4.2 convolution_convert_fusion
  275.1 39.8 %all-reduce.20.cloned.1.call-done = (bf16[3,608,256]{2,0,1:T(4,128)(2,1)}, bf16[3,608,256]{2,0,1:T(4,128)(2,1)}) async-done(((bf16[3,608,256]{2,0,1:T(4,128)(2,1)}, bf16[3,608,256]{2,0,1:T(4,128)(2,1)}), (bf16[3,608,256]{2,0,1:T(4,128)(2,1)}, bf16[3,608,256]{2,0,1:T(4,128)(2,1)})) %all-reduce.20.cloned.1.call-update) | async-done | bytes 1867792
  325.9 6.3 %reduce-scatter.7.cloned.1.call-done = bf16[256,512]{1,0:T(8,128)(2,1)} async-done(((bf16[256,1024]{1,0:T(8,128)(2,1)}), bf16[256,512]{1,0:T(8,128)(2,1)}) %reduce-scatter.7.cloned.1.call-update) | async-done | bytes 262160 | tf_op jit(solution)/shard_map/reduce_scatter | solution.py:191
  332.3 34.8 %reduce-scatter.9.cloned.1.call-done = bf16[512,1024]{1,0:T(8,128)(2,1)} async-done(((bf16[1024,1024]{1,0:T(8,128)(2,1)}), bf16[512,1024]{1,0:T(8,128)(2,1)}) %reduce-scatter.9.cloned.1.call-update) | async-done | bytes 1048592 | tf_op jit(solution)/shard_map/reduce_scatter | solution.py:194
  367.0 34.2 %reduce-scatter.11.cloned.1.call-done = bf16[1024,512]{1,0:T(8,128)(2,1)} async-done(((bf16[1024,1024]{1,0:T(8,128)(2,1)}), bf16[1024,512]{1,0:T(8,128)(2,1)}) %reduce-scatter.11.cloned.1.call-update) | async-done | bytes 1048592 | tf_op jit(solution)/shard_map/reduce_scatter | solution.py:197
  401.2 29.0 %reduce-scatter.5.cloned.1.call-done = bf16[3,512,256]{1,2,0:T(8,128)(2,1)} async-done(((bf16[3,1024,256]{1,2,0:T(8,128)(2,1)}), bf16[3,512,256]{1,2,0:T(8,128)(2,1)}) %reduce-scatter.5.cloned.1.call-update) | async-done | bytes 786448 | tf_op jit(solution)/shard_map/reduce_scatter | solution.py:188
  431.7 80.7 %all-reduce.16.cloned.1.call-done = (bf16[456,1024]{1,0:T(8,128)(2,1)}, bf16[456,1024]{1,0:T(8,128)(2,1)}) async-done(((bf16[456,1024]{1,0:T(8,128)(2,1)}, bf16[456,1024]{1,0:T(8,128)(2,1)}), (bf16[456,1024]{1,0:T(8,128)(2,1)}, bf16[456,1024]{1,0:T(8,128)(2,1)})) %all-reduce.16.cloned.1.call-update) | async-done | bytes 1867792 | tf_op jit(solution)/shard_map/psum | solution.py:119
  515.1 24.2 %all-reduce.2 = (f32[2,256]{1,0:T(2,128)}, f32[1024]{0:T(1024)}, f32[1024]{0:T(1024)}, f32[1024]{0:T(1024)}, f32[1024]{0:T(1024)}, /*index=5*/f32[1024]{0:T(1024)}, f32[1024]{0:T(1024)}, f32[1024]{0:T(1024)}) all-reduce(f32[2,256]{1,0:T(2,128)S(1)} %pad_maximum_fusion.3, ...), channel_id=1, replica_groups=mesh['shard'=2,'ctx'=4,'tp'=4] {'shard','ctx'}, use_global_device_ids=true, to_apply=%region_21.22 | all-reduce | flops 7680 | bytes 61440 | tf_op jit(solution)/shard_map/psum | solution.py:168
  539.4 4.5 fusion.13
  543.9 39.1 %all-reduce.18.cloned.1.call-done = (bf16[3,512,256]{1,2,0:T(8,128)(2,1)}, bf16[256,512]{1,0:T(8,128)(2,1)}, bf16[512,1024]{1,0:T(8,128)(2,1)}, bf16[1024,512]{1,0:T(8,128)(2,1)}) async-done(((bf16[3,512,256]{1,2,0:T(8,128)(2,1)}, bf16[256,512]{1,0:T(8,128)(2,1)}, bf16[512,1024]{1,0:T(8,128)(2,1)}, bf16[1024,512]{1,0:T(8,128)(2,1)}), (bf16[3,512,256]{1,2,0:T(8,128)(2,1)}, bf16[256,512]{1,0:T(8,128)(2,1)}, ...) | async-done | bytes 3145744 | tf_op jit(solution)/shard_map/psum | solution.py:182
  (161 shorter events, 84.4 us)
Async XLA Ops:
  7.2 24.5 %copy-start.24 = (f32[1024]{0:T(1024)S(1)}, f32[1024]{0:T(1024)}, u32[]{:S(2)}) copy-start(f32[1024]{0:T(1024)} %param.17) | copy-start | bytes 12292
  7.2 24.5 %copy-start.28 = (f32[1024]{0:T(1024)S(1)}, f32[1024]{0:T(1024)}, u32[]{:S(2)}) copy-start(f32[1024]{0:T(1024)} %param.18) | copy-start | bytes 12292
  7.2 36.5 %all-gather.4.cloned.1.call-start = ((), (), s32[]{:S(2)}) async-start(), calls=%async_computation.4 | async-start | bytes 2359296 | tf_op jit(solution)/shard_map/all_gather | solution.py:66
  8.0 124.1 %all-reduce.12.cloned.1.call-start = ((), (), s32[]{:S(2)}) async-start(), calls=%async_computation.5 | async-start | bytes 1867776 | tf_op jit(solution)/shard_map/psum | solution.py:112
  33.3 12.7 %copy-start.20 = (bf16[456,1024]{1,0:T(8,128)(2,1)}, bf16[456,1024]{1,0:T(8,128)(2,1)S(1)}, u32[]{:S(2)}) copy-start(bf16[456,1024]{1,0:T(8,128)(2,1)S(1)} %get-tuple-element.101) | copy-start | bytes 2801668
  51.2 25.2 %copy-start.6 = (bf16[3,152,4,64]{1,3,2,0:T(8,128)(2,1)}, bf16[3,152,4,64]{1,3,2,0:T(8,128)(2,1)S(1)}, u32[]{:S(2)}) copy-start(bf16[3,152,4,64]{1,3,2,0:T(8,128)(2,1)S(1)} %copy.66) | copy-start | bytes 700420
  64.2 12.2 %copy-start.4 = (bf16[3,608,256]{1,2,0:T(8,128)(2,1)}, bf16[3,608,256]{1,2,0:T(8,128)(2,1)S(1)}, u32[]{:S(2)}) copy-start(bf16[3,608,256]{1,2,0:T(8,128)(2,1)S(1)} %copy.65) | copy-start | bytes 2801668
  81.8 31.1 %copy-start.13 = (bf16[456,256]{1,0:T(8,128)(2,1)}, bf16[456,256]{1,0:T(8,128)(2,1)S(1)}, u32[]{:S(2)}) copy-start(bf16[456,256]{1,0:T(8,128)(2,1)S(1)} %reshape.158) | copy-start | bytes 700420
  83.1 82.8 %all-gather.6.cloned.1.call-start = ((), (), s32[]{:S(2)}) async-start(), calls=%async_computation.6 | async-start | bytes 3145728 | tf_op jit(solution)/shard_map/all_gather | solution.py:70
  83.2 25.6 %collective-permute-start = (bf16[1024,512]{1,0:T(8,128)(2,1)S(1)}, bf16[1024,512]{1,0:T(8,128)(2,1)}, u32[]{:S(2)}, u32[]{:S(2)}) collective-permute-start(bf16[1024,512]{1,0:T(8,128)(2,1)S(1)} %copy-done.17), channel_id=1, source_target_pairs={{0,16},{16,0},{1,17},{17,1},{2,18},{18,2},{3,19},{19,3},{4,20},{20... | collective-permute-start | bytes 3145736 | tf_op jit(solution)/shard_map/ppermute | solution.py:16
  84.7 142.7 %all-reduce.14.cloned.1.call-start = ((), (), s32[]{:S(2)}) async-start(), calls=%async_computation.7 | async-start | bytes 1867776 | tf_op jit(solution)/shard_map/psum | solution.py:130
  112.9 20.7 %copy-start.23 = (f32[1024]{0:T(1024)S(1)}, f32[1024]{0:T(1024)}, u32[]{:S(2)}) copy-start(f32[1024]{0:T(1024)} %param.22) | copy-start | bytes 12292
  134.8 31.1 %copy-start.25 = (f32[1024]{0:T(1024)S(1)}, f32[1024]{0:T(1024)}, u32[]{:S(2)}) copy-start(f32[1024]{0:T(1024)} %param.23) | copy-start | bytes 12292
  134.8 31.1 %copy-start.31 = (f32[1024]{0:T(1024)S(1)}, f32[1024]{0:T(1024)}, u32[]{:S(2)}) copy-start(f32[1024]{0:T(1024)} %param.26) | copy-start | bytes 12292
  134.8 31.1 %copy-start.32 = (f32[1024]{0:T(1024)S(1)}, f32[1024]{0:T(1024)}, u32[]{:S(2)}) copy-start(f32[1024]{0:T(1024)} %param.24) | copy-start | bytes 12292
  135.2 92.2 %copy-start.3 = (f32[456,1024]{1,0:T(8,128)}, f32[456,1024]{1,0:T(8,128)S(1)}, u32[]{:S(2)}) copy-start(f32[456,1024]{1,0:T(8,128)S(1)} %subtract_multiply_fusion) | copy-start | bytes 5603332
  178.6 136.2 %all-reduce.20.cloned.1.call-start = ((), (), s32[]{:S(2)}) async-start(), calls=%async_computation.14 | async-start | bytes 4980736
  257.7 74.5 %reduce-scatter.7.cloned.1.call-start = ((), (), s32[]{:S(2)}) async-start(), calls=%async_computation.9 | async-start | bytes 786432 | tf_op jit(solution)/shard_map/reduce_scatter | solution.py:191
  259.1 107.9 %reduce-scatter.9.cloned.1.call-start = ((), (), s32[]{:S(2)}) async-start(), calls=%async_computation.10 | async-start | bytes 3145728 | tf_op jit(solution)/shard_map/reduce_scatter | solution.py:194
  263.5 137.6 %reduce-scatter.11.cloned.1.call-start = ((), (), s32[]{:S(2)}) async-start(), calls=%async_computation.11 | async-start | bytes 3145728 | tf_op jit(solution)/shard_map/reduce_scatter | solution.py:197
  267.8 162.4 %reduce-scatter.5.cloned.1.call-start = ((), (), s32[]{:S(2)}) async-start(), calls=%async_computation.8 | async-start | bytes 2359296 | tf_op jit(solution)/shard_map/reduce_scatter | solution.py:188
  319.6 192.7 %all-reduce.16.cloned.1.call-start = ((), (), s32[]{:S(2)}) async-start(), calls=%async_computation.12 | async-start | bytes 3735552 | tf_op jit(solution)/shard_map/psum | solution.py:119
  325.9 257.1 %all-reduce.18.cloned.1.call-start = ((), (), s32[]{:S(2)}) async-start(), calls=%async_computation.13 | async-start | bytes 6291456 | tf_op jit(solution)/shard_map/psum | solution.py:182
  512.3 27.0 %copy-start.26 = (f32[1024]{0:T(1024)S(1)}, f32[1024]{0:T(1024)}, u32[]{:S(2)}) copy-start(f32[1024]{0:T(1024)} %param.28) | copy-start | bytes 12292
  (23 other events, 80.1 us)
Sparse Core Ops, SparseCore 0:
  9.6 34.1 all-gather.3
  83.3 48.7 all-reduce.11
  133.6 32.2 all-gather.5
  178.7 48.6 all-reduce.13
  257.9 56.9 all-reduce.19
  317.5 14.6 reduce-scatter.6
  335.1 31.8 reduce-scatter.8
  369.2 31.8 reduce-scatter.10
  404.0 26.1 reduce-scatter.4
  433.6 78.6 all-reduce.15
  514.9 67.9 all-reduce.17
